TPU v7x, 32 devices: a whole 2x2x4 slice. The times are simulated.
32 devices in a mesh: rep: 2 (over x), seq: 8 (over z, y), tp: 2 (over core).
Axes of the slice: x: 2, y: 2, z: 4, core: 2. Of those that a mesh axis runs over, the one named last changes fastest.
Arguments:
- prefill_query: bfloat16 [8192, 2048], P(('rep', 'seq'), 'tp'), parts along dimension 0, may hold values from -50 to 50
- prefill_key: bfloat16 [8192, 512], P(('rep', 'seq'), 'tp'), parts along dimension 0, may hold values from -6 to 6
- prefill_value: bfloat16 [8192, 512], P(('rep', 'seq'), 'tp'), parts along dimension 0, may hold values from -6 to 6
- doc_ids: int32 [8192], P('rep'), parts along dimension 0, may hold values from 0 to 3, never falling along the last dimension, each value on 1 to 2048 neighbouring positions
- head_window: int32 [16], P('tp'), may hold values from 1024 to 4096, as said below
- dec_query: bfloat16 [128, 2048], P('rep', 'tp'), parts along dimension 0, may hold values from -50 to 50
- dec_key: bfloat16 [128, 512], P('rep', 'tp'), parts along dimension 0, may hold values from -6 to 6
- dec_value: bfloat16 [128, 512], P('rep', 'tp'), parts along dimension 0, may hold values from -6 to 6
- cache_key: bfloat16 [65536, 512], P(('rep', 'seq'), 'tp'), parts along dimension 0, may hold values from -6 to 6
- cache_value: bfloat16 [65536, 512], P(('rep', 'seq'), 'tp'), parts along dimension 0, may hold values from -6 to 6
- page_order: int32 [512], P(('rep', 'seq')), parts along dimension 0, may hold values from 0 to 255, each once
- lengths: int32 [128], P('rep'), parts along dimension 0, may hold values from 1 to 512, 16384 in all
- out_proj: bfloat16 [2048, 4096], P('tp'), may hold values from -0.125 to 0.125
Outputs:
- prompt_out: bfloat16 [8192, 4096], P(('rep', 'seq', 'tp')), parts along dimension 0
- decode_out: bfloat16 [128, 4096], P(('rep', 'tp')), parts along dimension 0
There are 2 independent parts, one for each index of `rep`. A program takes and returns all parts, laid end to end along the dimension named above; an argument that names none is the same for every part. Nothing has to cross between parts.
Inputs may be any that keep to these rules, and one draw needn't show every extreme that they name: `head_window`: some head has window 4096.
All inputs are finite; a program needn't handle non-finite values.
Results may differ from a plain program's by a relative error of at most 0.015.
Values may be sent and summed in bfloat16 or wider, within the bound.
A program may use at most 256 MiB of HBM per device.

v0:
```python
import functools
import math

import jax
import jax.numpy as jnp
from jax import lax
from jax.experimental import pallas as pl
from jax.experimental.pallas import tpu as pltpu
from jax.sharding import PartitionSpec as P

HD = 128
WINDOW = 4096
PAGE = 128
DOCS = 4
MASKED = -1e30
FLOOR = -1e29
NEAR = WINDOW // 4
SUB = 256
SPAN = 2
MESH = pl.DeviceIdType.MESH


def dot_t(a, b):
    return lax.dot_general(a, b, (((1,), (1,)), ((), ())), preferred_element_type=jnp.float32)


def wide(column, width):
    return jnp.concatenate([column] * (width // column.shape[1]), axis=1)


def put(block_p, block_d, out_p, out_d, sem):
    copies = [
        pltpu.make_async_copy(block_p, out_p, sem.at[0]),
        pltpu.make_async_copy(block_d, out_d, sem.at[1]),
    ]
    for copy in copies:
        copy.start()
    for copy in copies:
        copy.wait()


def kernel(
    n, back, reach, pages_request, q_hbm, k_hbm, v_hbm, docs_hbm, windows, order, lengths,
    dq_hbm, dk_hbm, dv_hbm, ck, cv, w,
    out_p, out_d,
    q, k, v, docs, dq, dk, dv,
    kv, top, acc, lo, rows, ckv, cvv, wv, spread, pieces, part, stats, gathered, gathered_stats,
    att, outgoing, incoming,
    local_sem, zs, zr, ys, yr, ps, pr, fs, fr, ts, tr,
):
    me = lax.axis_index("seq")
    core = lax.axis_index("tp")
    other = 1 - core
    odd = lax.rem(me, 2)
    partner = me + 1 - 2 * odd
    tokens = q.shape[0]
    heads = q.shape[1] // HD
    groups = k.shape[1] // HD
    per = heads // groups
    reqs = dq.shape[0]
    pages = order.shape[0]
    owned = heads // SPAN
    scale = 1.0 / math.sqrt(HD)
    exp_scale = scale * math.log2(math.e)

    pairs = (
        (k_hbm, k), (v_hbm, v), (q_hbm, q), (docs_hbm, docs), (dq_hbm, dq), (ck, ckv), (cv, cvv),
        (dk_hbm, dk), (dv_hbm, dv), (w, wv),
    )
    loads = [pltpu.make_async_copy(a, b, local_sem.at[i]) for i, (a, b) in enumerate(pairs)]
    for load in loads:
        load.start()

    barrier = pltpu.get_barrier_semaphore()

    def greet(d, carry):
        pl.semaphore_signal(
            barrier, inc=1, device_id={"seq": lax.rem(me + d, n)}, device_id_type=MESH
        )
        return carry

    lax.fori_loop(1, n, greet, 0)
    pl.semaphore_signal(barrier, inc=1, device_id={"tp": other}, device_id_type=MESH)
    pl.semaphore_wait(barrier, n)

    def source(s, g, i):
        if s == 0:
            return (k, v)[i].at[:, pl.ds(g * HD, HD)]
        return kv.at[s - 1, g, i]

    def along(s, g, i):
        return pltpu.make_async_remote_copy(
            src_ref=source(s, g, i),
            dst_ref=kv.at[s + 1, g, i],
            send_sem=zs.at[s // 2, g, i],
            recv_sem=zr.at[s // 2, g, i],
            device_id={"seq": lax.rem(me + 2, n)},
            device_id_type=MESH,
        )

    def across(s, h, g, i):
        return pltpu.make_async_remote_copy(
            src_ref=source(s, g, i),
            dst_ref=kv.at[2 * h - 2, g, i],
            send_sem=ys.at[h - 1, g, i],
            recv_sem=yr.at[h - 1, g, i],
            device_id={"seq": partner},
            device_id_type=MESH,
        )

    def forward(s, g, finish=False, only=(0, 1)):
        act = (lambda c: c.wait_send()) if finish else (lambda c: c.start())
        if s + 2 <= back:
            @pl.when((me >= s) & (me + 2 < n))
            def _():
                for i in only:
                    act(along(s, g, i))

            @pl.when((me >= s) & (odd == 0))
            def _():
                for i in only:
                    act(across(s, s // 2 + 1, g, i))
        if s >= 2:
            @pl.when((me >= s) & (odd == 1))
            def _():
                for i in only:
                    act(across(s, s // 2, g, i))

    def arrive(s, g):
        @pl.when(me >= s)
        def _():
            for i in range(2):
                if s % 2 == 0:
                    along(s - 2, g, i).wait_recv()
                else:
                    across(s + 1, (s + 1) // 2, g, i).wait_recv()

        if s % 2 == 0:
            forward(s, g)

    def attend(s, g):
        def one_head(head):
            lanes = slice(g * HD, (g + 1) * HD)
            keys = k[:, lanes] if s == 0 else kv[s - 1, g, 0]
            values = v[:, lanes] if s == 0 else kv[s - 1, g, 1]
            values = jnp.concatenate([values, jnp.ones_like(values)], axis=1)
            size = math.gcd(tokens, SUB)
            for r in range(0, tokens, size):
                cut = slice(r, r + size)
                first = max(0, (s * tokens + r - reach + 1) // HD * HD)
                last = r + size if s == 0 else tokens
                span = last - first
                queries = q[cut, head * HD:(head + 1) * HD]
                scores = dot_t(queries, keys[first:last])
                limit = lo[cut]
                if (s + 1) * tokens > NEAR:
                    place = me * tokens + r + lax.broadcasted_iota(jnp.int32, (size, HD), 0)
                    limit = jnp.maximum(limit, place - windows[head] + 1)
                limit = limit - ((me - s) * tokens + first)
                column = lax.broadcasted_iota(jnp.int32, (size, span), 1)
                allowed = column >= wide(limit, span)
                if s == 0:
                    allowed = allowed & (
                        column <= lax.broadcasted_iota(jnp.int32, (size, span), 0) + r
                    )
                scores = jnp.where(allowed, scores, MASKED)
                high = jnp.max(scores, axis=1, keepdims=True) * exp_scale
                high = jnp.broadcast_to(high, (size, HD))
                if s > 0:
                    old = top[head, cut]
                    high = jnp.maximum(high, old)
                weights = jnp.exp2(scores * exp_scale - wide(high, span))
                added = jnp.dot(
                    weights.astype(jnp.bfloat16), values[first:last],
                    preferred_element_type=jnp.float32,
                )
                if s > 0:
                    added = added + acc[head, cut] * wide(jnp.exp2(old - high), 2 * HD)
                top[head, cut] = high
                acc[head, cut] = added

        @pl.when(me >= s)
        def _():
            for r in range(per):
                one_head(g * per + r)

    def to_owner(owner):
        return [
            pltpu.make_async_remote_copy(
                src_ref=src,
                dst_ref=dst.at[me],
                send_sem=ps.at[owner, i],
                recv_sem=pr.at[me, i],
                device_id={"seq": owner},
                device_id_type=MESH,
            )
            for i, (src, dst) in enumerate(
                ((part.at[pl.ds(owner * owned, owned)], gathered), (stats, gathered_stats))
            )
        ]

    def decode_partials():
        for i in (4, 5, 6):
            loads[i].wait()
        spread[...] = jnp.zeros_like(spread)
        for head in range(heads):
            g = head // per
            spread[:, head, g * HD:(g + 1) * HD] = (
                dq[:, head * HD:(head + 1) * HD].astype(jnp.float32)
            )
        step = math.gcd(pages, 8)
        lane = lax.broadcasted_iota(jnp.int32, (heads, PAGE), 1)
        group = lax.broadcasted_iota(jnp.int32, (heads, HD), 0) // per

        def block(b, carry):
            levels, owners = carry
            scores, spans, who = [], [], []
            for i in range(step):
                page = order[b * step + i]
                owner = page // pages_request
                left = lengths[owner] - (page - owner * pages_request) * PAGE
                span = pl.ds(pl.multiple_of((b * step + i) * PAGE, PAGE), PAGE)
                score = dot_t(spread[owner].astype(jnp.bfloat16), ckv[span, :])
                scores.append(jnp.where(lane < left, score, MASKED))
                spans.append(span)
                who.append(owner)
            scores = jnp.concatenate(scores, axis=0)
            high = jnp.max(scores, axis=1, keepdims=True)
            high = jnp.broadcast_to(jnp.maximum(high, FLOOR) * exp_scale, scores.shape)
            weights = jnp.exp2(scores * exp_scale - high)
            total = jnp.broadcast_to(jnp.sum(weights, axis=1, keepdims=True), scores.shape)
            some = total > 0.0
            whole = jnp.where(some, total, 1.0)
            level = jnp.where(some, high + jnp.log2(whole), FLOOR)
            weights = (weights / whole).astype(jnp.bfloat16)
            for i in range(step):
                cut = slice(i * heads, (i + 1) * heads)
                both = jnp.dot(
                    weights[cut], cvv[spans[i], :], preferred_element_type=jnp.float32
                )
                mixed = both[:, :HD]
                for g in range(1, groups):
                    mixed = jnp.where(group == g, both[:, g * HD:(g + 1) * HD], mixed)
                pieces[b * step + i] = mixed
                here = lane == b * step + i
                levels = jnp.where(here, level[cut], levels)
                owners = jnp.where(here, who[i].astype(jnp.float32), owners)
            return (levels, owners)

        blank = jnp.zeros((heads, PAGE), jnp.float32)
        levels, owners = lax.fori_loop(
            0, pages // step, block, (blank + FLOOR, blank - 1.0)
        )
        stats[:heads] = levels
        stats[heads:] = owners
        for head in range(heads):
            part[head] = pieces[:, head].astype(jnp.bfloat16)
        for owner in range(SPAN):
            @pl.when(me != owner)
            def _():
                for copy in to_owner(owner):
                    copy.start()

    def decode_merge():
        @pl.when(me < SPAN)
        def _():
            loads[7].wait()
            loads[8].wait()
            gathered[me] = part[pl.ds(me * owned, owned)]
            gathered_stats[me] = stats[...]

            def take(d, carry):
                j = lax.rem(me + d, n)
                for i, (src, dst) in enumerate(
                    ((part.at[pl.ds(0, owned)], gathered), (stats, gathered_stats))
                ):
                    pltpu.make_async_remote_copy(
                        src_ref=src,
                        dst_ref=dst.at[j],
                        send_sem=ps.at[0, i],
                        recv_sem=pr.at[j, i],
                        device_id={"seq": partner},
                        device_id_type=MESH,
                    ).wait_recv()
                return carry

            lax.fori_loop(1, n, take, 0)
            request = lax.broadcasted_iota(jnp.int32, (reqs, PAGE), 0).astype(jnp.float32)

            def one_head(r, carry):
                head = me * owned + r
                queries = dq[:, pl.ds(pl.multiple_of(head * HD, HD), HD)].astype(jnp.float32)
                group = pl.ds(pl.multiple_of((head // per) * HD, HD), HD)
                own = jnp.sum(queries * dk[:, group].astype(jnp.float32), axis=1, keepdims=True)
                own = jnp.broadcast_to(own * exp_scale, (reqs, HD))
                levels = []
                high = own
                for j in range(n):
                    level = gathered_stats[j, pl.ds(head, 1), :]
                    level = jnp.where(gathered_stats[j, heads:heads + 1, :] == request, level, FLOOR)
                    levels.append(level)
                    high = jnp.maximum(
                        high, jnp.broadcast_to(jnp.max(level, axis=1, keepdims=True), high.shape)
                    )
                mine = jnp.exp2(own - high)
                summed = mine * dv[:, group].astype(jnp.float32)
                total = jnp.zeros((reqs, PAGE), jnp.float32)
                for j in range(n):
                    weight = jnp.exp2(levels[j] - high)
                    total = total + weight
                    summed = summed + jnp.dot(
                        weight[:, :pages].astype(jnp.bfloat16), gathered[j, r],
                        preferred_element_type=jnp.float32,
                    )
                total = mine + jnp.broadcast_to(
                    jnp.sum(total, axis=1, keepdims=True), mine.shape
                )
                att[head] = (summed / total).astype(jnp.bfloat16)
                return carry

            lax.fori_loop(0, owned, one_head, 0)

    def finals(i, half=None):
        half = pl.ds((odd if half is None else half) * owned, owned)
        return pltpu.make_async_remote_copy(
            src_ref=att.at[half],
            dst_ref=att.at[half],
            send_sem=fs.at[i],
            recv_sem=fr.at[i],
            device_id={"seq": partner if i else lax.rem(me + 2, n)},
            device_id_type=MESH,
        )

    def relay(level):
        @pl.when(me // SPAN == level)
        def _():
            if level:
                finals(0).wait_recv()

            @pl.when(me + 2 < n)
            def _():
                finals(0).start()

            finals(1).start()

    for i in (0, 1):
        loads[i].wait()
    for g in range(groups):
        forward(0, g)
    loads[3].wait()
    position = me * tokens + lax.broadcasted_iota(jnp.int32, (tokens, HD), 0)
    place = position.astype(jnp.float32)
    start = jnp.zeros((tokens, HD), jnp.float32)
    for document in range(1, DOCS):
        before = (docs[...] < document).astype(jnp.float32)
        before = jnp.sum(jnp.sum(before, axis=0, keepdims=True), axis=1, keepdims=True)
        start = jnp.where(before <= place, jnp.maximum(start, before), start)
    lo[...] = start.astype(jnp.int32)
    decode_partials()
    loads[2].wait()
    for g in range(groups):
        attend(0, g)
    for g in range(groups):
        arrive(2, g)
        attend(2, g)
    decode_merge()
    relay(0)
    relay(1)
    levels = n // SPAN
    for h in range(1, back // 2 + 1):
        for g in range(groups):
            if 2 * h + 2 <= back:
                arrive(2 * h + 2, g)
            arrive(2 * h - 1, g)
            attend(2 * h - 1, g)
            if h == 1 and g == 0 and levels > 2:
                relay(2)
            if h == 1 and g == groups - 1:
                for level in range(3, levels):
                    relay(level)
        if 2 * h + 2 <= back:
            for g in range(groups):
                attend(2 * h + 2, g)

    half = tokens // 2
    half_reqs = reqs // 2
    finals(1, 1 - odd).wait_recv()
    for head in range(heads):
        cut = slice(head * HD, (head + 1) * HD)
        done = (acc[head, :, :HD] / acc[head, :, HD:]).astype(jnp.bfloat16)
        for c in range(2):
            rows[c, :half, cut] = done[c * half:(c + 1) * half]
            rows[c, half:, cut] = att[head, c * half_reqs:(c + 1) * half_reqs]

    loads[9].wait()
    blocks = outgoing.shape[0]
    width = outgoing.shape[2]

    def exchange(b):
        return pltpu.make_async_remote_copy(
            src_ref=outgoing.at[b],
            dst_ref=incoming.at[b],
            send_sem=ts.at[b],
            recv_sem=tr.at[b],
            device_id={"tp": other},
            device_id_type=MESH,
        )

    def project(c, b):
        span = pl.ds(pl.multiple_of(b * width, width), width)
        return jnp.dot(rows[c], wv[:, span], preferred_element_type=jnp.float32)

    def give(b, carry):
        outgoing[b] = project(other, b).astype(jnp.bfloat16)
        exchange(b).start()
        return carry

    def keep(b, carry):
        own = project(core, b).astype(jnp.bfloat16).astype(jnp.float32)
        exchange(b).wait_recv()
        total = (own + incoming[b].astype(jnp.float32)).astype(jnp.bfloat16)
        span = pl.ds(pl.multiple_of(b * width, width), width)
        out_p[:, span] = total[:half]
        out_d[:, span] = total[half:]
        return carry

    lax.fori_loop(0, blocks, give, 0)
    lax.fori_loop(0, blocks, keep, 0)

    def sent(b, carry):
        exchange(b).wait_send()
        return carry

    lax.fori_loop(0, blocks, sent, 0)
    for s in range(0, back + 1, 2):
        for g in range(groups):
            forward(s, g, finish=True)
    for owner in range(SPAN):
        @pl.when(me != owner)
        def _():
            for copy in to_owner(owner):
                copy.wait_send()

    @pl.when(me + 2 < n)
    def _():
        finals(0).wait_send()

    finals(1).wait_send()

    @pl.when(me >= SPAN)
    def _():
        loads[7].wait()
        loads[8].wait()


def on_device(
    n, prefill_query, prefill_key, prefill_value, doc_ids, head_window, dec_query, dec_key,
    dec_value, cache_key, cache_value, page_order, lengths, out_proj,
):
    tokens, width = prefill_query.shape
    heads = width // HD
    groups = prefill_key.shape[1] // HD
    reqs = dec_query.shape[0]
    model = out_proj.shape[1]
    pages = page_order.shape[0]
    reach = min(doc_ids.shape[0] // 2, WINDOW)
    back = -(-reach // tokens)
    back += back % 2

    pages_request = page_order.shape[0] * n // reqs
    docs = doc_ids.reshape(-1, HD)
    vmem = pl.BlockSpec(memory_space=pltpu.VMEM)
    hbm = pl.BlockSpec(memory_space=pltpu.HBM)
    smem = pl.BlockSpec(memory_space=pltpu.SMEM)
    block = 512
    blocks = model // block
    merged = (tokens + reqs) // 2
    dma = pltpu.SemaphoreType.DMA
    args = (
        prefill_query, prefill_key, prefill_value, docs, head_window, page_order, lengths,
        dec_query, dec_key, dec_value, cache_key, cache_value, out_proj,
    )
    result = pl.pallas_call(
        functools.partial(kernel, n, back, reach, pages_request),
        out_shape=(
            jax.ShapeDtypeStruct((tokens // 2, model), jnp.bfloat16),
            jax.ShapeDtypeStruct((reqs // 2, model), jnp.bfloat16),
        ),
        in_specs=[hbm] * 4 + [smem] * 3 + [hbm] * 6,
        out_specs=(vmem, vmem),
        scratch_shapes=[
            pltpu.VMEM(prefill_query.shape, jnp.bfloat16),
            pltpu.VMEM(prefill_key.shape, jnp.bfloat16),
            pltpu.VMEM(prefill_value.shape, jnp.bfloat16),
            pltpu.VMEM(docs.shape, jnp.int32),
            pltpu.VMEM(dec_query.shape, jnp.bfloat16),
            pltpu.VMEM(dec_key.shape, jnp.bfloat16),
            pltpu.VMEM(dec_value.shape, jnp.bfloat16),
            pltpu.VMEM((back, groups, 2, tokens, HD), jnp.bfloat16),
            pltpu.VMEM((heads, tokens, HD), jnp.float32),
            pltpu.VMEM((heads, tokens, 2 * HD), jnp.float32),
            pltpu.VMEM((tokens, HD), jnp.int32),
            pltpu.VMEM((2, merged, heads * HD), jnp.bfloat16),
            pltpu.VMEM(cache_key.shape, jnp.bfloat16),
            pltpu.VMEM(cache_value.shape, jnp.bfloat16),
            pltpu.VMEM(out_proj.shape, jnp.bfloat16),
            pltpu.VMEM((reqs, heads, groups * HD), jnp.float32),
            pltpu.VMEM((pages, heads, HD), jnp.float32),
            pltpu.VMEM((heads, pages, HD), jnp.bfloat16),
            pltpu.VMEM((2 * heads, PAGE), jnp.float32),
            pltpu.VMEM((n, heads // SPAN, pages, HD), jnp.bfloat16),
            pltpu.VMEM((n, 2 * heads, PAGE), jnp.float32),
            pltpu.VMEM((heads, reqs, HD), jnp.bfloat16),
            pltpu.VMEM((blocks, merged, block), jnp.bfloat16),
            pltpu.VMEM((blocks, merged, block), jnp.bfloat16),
            dma((10,)),
            dma((back // 2, groups, 2)),
            dma((back // 2, groups, 2)),
            dma((back // 2, groups, 2)),
            dma((back // 2, groups, 2)),
            dma((SPAN, 2)),
            dma((n, 2)),
            dma((2,)),
            dma((2,)),
            dma((blocks,)),
            dma((blocks,)),
        ],
        compiler_params=pltpu.CompilerParams(
            collective_id=0, has_side_effects=True, vmem_limit_bytes=48 * 1024 * 1024
        ),
    )(*[pltpu.with_memory_space_constraint(x, pltpu.HBM) for x in args])
    return pl.pallas_call(
        put,
        out_shape=tuple(jax.ShapeDtypeStruct(x.shape, x.dtype) for x in result),
        in_specs=[vmem, vmem],
        out_specs=(hbm, hbm),
        scratch_shapes=[dma((2,))],
        compiler_params=pltpu.CompilerParams(vmem_limit_bytes=4 * 1024 * 1024),
    )(*result)


def solution(mesh):
    placed = (
        P(("rep", "seq"), "tp"),
        P(("rep", "seq"), "tp"),
        P(("rep", "seq"), "tp"),
        P("rep"),
        P("tp"),
        P("rep", "tp"),
        P("rep", "tp"),
        P("rep", "tp"),
        P(("rep", "seq"), "tp"),
        P(("rep", "seq"), "tp"),
        P(("rep", "seq")),
        P("rep"),
        P("tp", None),
    )
    return jax.shard_map(
        functools.partial(on_device, mesh.shape["seq"]),
        mesh=mesh,
        in_specs=placed,
        out_specs=(P(("rep", "seq", "tp"), None), P(("rep", "tp"), None)),
        check_vma=False,
    )
```

profile of v0, /device:TPU:16, one launch (start us, length us, event | category | flops | bytes accessed | tf_op | source)
XLA Modules:
  0.0 49.9 jit_solution(596562862706297028)
XLA Ops:
  0.6 47.7 %shard_map.140 = (bf16[256,4096]{1,0:T(8,128)(2,1)S(1)}, bf16[32,4096]{1,0:T(8,128)(2,1)S(1)}) custom-call(bf16[512,1024]{1,0:T(8,128)(2,1)} %q_hbm.1, bf16[512,256]{1,0:T(8,128)(2,1)} %k_hbm.1, bf16[512,256]{1,0:T(8,128)(2,1)} %v_hbm.1, s32[32,128]{1,0:T(8,128)} %bitcast.1, s32[8]{0:T(128)} %windows.1, s32[32]{0:T(128)} %order.1, s32[64]{0:T(128)} %lengths.1, ...), custom_call_target="tpu_custom_call" | custom-call | tf_op jit(solution)/shard_map/pallas_call | solution.py:483
  48.4 1.4 %shard_map.141 = (bf16[256,4096]{1,0:T(8,128)(2,1)}, bf16[32,4096]{1,0:T(8,128)(2,1)}) custom-call(bf16[256,4096]{1,0:T(8,128)(2,1)S(1)} %get-tuple-element.4.block_p, bf16[32,4096]{1,0:T(8,128)(2,1)S(1)} %get-tuple-element.5.block_d), custom_call_target="tpu_custom_call" | custom-call | tf_op jit(solution)/shard_map/pallas_call | solution.py:532
where the time goes:
time: 50.6 us; the launch traced here: 49.9 us
  Pallas kernels  49.1 us (97%)
  between operations  0.8 us (2%)
    pallas_call x1, Pallas kernels, on_device(): pl.pallas_call(functools.partial(kernel, n, back, reach, pages_request),...  47.7 us
    pallas_call x1, Pallas kernels, on_device(): pl.pallas_call(put, out_shape=tuple((jax.ShapeDtypeStruct(x.shape, x.dtyp...  1.41 us

commit v1 on v0

v1 whole, which is shorter than its diff:
```python
import functools
import math

import jax
import jax.numpy as jnp
from jax import lax
from jax.experimental import pallas as pl
from jax.experimental.pallas import tpu as pltpu
from jax.sharding import PartitionSpec as P

HD = 128
WINDOW = 4096
PAGE = 128
DOCS = 4
MASKED = -1e30
FLOOR = -1e29
NEAR = WINDOW // 4
SUB = 256
CUTS = 2
MESH = pl.DeviceIdType.MESH


def dot_t(a, b):
    return lax.dot_general(a, b, (((1,), (1,)), ((), ())), preferred_element_type=jnp.float32)


def wide(column, width):
    return jnp.concatenate([column] * (width // column.shape[1]), axis=1)


def put(block_p, block_d, out_p, out_d, sem):
    copies = [
        pltpu.make_async_copy(block_p, out_p, sem.at[0]),
        pltpu.make_async_copy(block_d, out_d, sem.at[1]),
    ]
    for copy in copies:
        copy.start()
    for copy in copies:
        copy.wait()


def kernel(
    n, back, reach, pages_request, q_hbm, k_hbm, v_hbm, docs_hbm, windows, order, lengths,
    dq_hbm, dk_hbm, dv_hbm, ck, cv, w,
    out_p, out_d,
    q, k, v, docs, dq, dk, dv,
    kv, top, acc, lo, rows, ckv, cvv, wv, spread, pieces, part, stats, gathered, gathered_stats,
    att, total, wx, incoming,
    local_sem, zs, zr, ys, yr, ps, pr, fs, fr, ts, tr, ws, wr, gate,
):
    me = lax.axis_index("seq")
    core = lax.axis_index("tp")
    other = 1 - core
    odd = lax.rem(me, 2)
    partner = me + 1 - 2 * odd
    tokens = q.shape[0]
    heads = q.shape[1] // HD
    groups = k.shape[1] // HD
    per = heads // groups
    reqs = dq.shape[0]
    pages = order.shape[0]
    scale = 1.0 / math.sqrt(HD)
    exp_scale = scale * math.log2(math.e)

    pairs = (
        (k_hbm, k), (v_hbm, v), (dq_hbm, dq), (ck, ckv), (cv, cvv), (docs_hbm, docs), (q_hbm, q),
        (dk_hbm, dk), (dv_hbm, dv), (w, wv),
    )
    loads = [pltpu.make_async_copy(a, b, local_sem.at[i]) for i, (a, b) in enumerate(pairs)]
    for load in loads[:7]:
        load.start()

    barrier = pltpu.get_barrier_semaphore()

    @pl.when(me >= 2)
    def _():
        pl.semaphore_signal(barrier, inc=1, device_id={"seq": me - 2}, device_id_type=MESH)

    pl.semaphore_signal(barrier, inc=1, device_id={"seq": partner}, device_id_type=MESH)
    pl.semaphore_signal(barrier, inc=1, device_id={"tp": other}, device_id_type=MESH)
    pl.semaphore_wait(barrier, 2 + (me + 2 < n).astype(jnp.int32))

    def pass_gate():
        @pl.when(me >= 2)
        def _():
            pl.semaphore_wait(gate, 1)

        @pl.when(me + 2 < n)
        def _():
            pl.semaphore_signal(gate, inc=1, device_id={"seq": me + 2}, device_id_type=MESH)

    piece = tokens // CUTS

    def source(s, g, i, c):
        span = pl.ds(c * piece, piece)
        if s == 0:
            return (k, v)[i].at[span, pl.ds(g * HD, HD)]
        return kv.at[s - 1, g, i, span]

    def along(s, g, i, c):
        return pltpu.make_async_remote_copy(
            src_ref=source(s, g, i, c),
            dst_ref=kv.at[s + 1, g, i, pl.ds(c * piece, piece)],
            send_sem=zs.at[s // 2, g, i, c],
            recv_sem=zr.at[s // 2, g, i, c],
            device_id={"seq": lax.rem(me + 2, n)},
            device_id_type=MESH,
        )

    def across(s, h, g, i, c):
        return pltpu.make_async_remote_copy(
            src_ref=source(s, g, i, c),
            dst_ref=kv.at[2 * h - 2, g, i, pl.ds(c * piece, piece)],
            send_sem=ys.at[h - 1, g, i, c],
            recv_sem=yr.at[h - 1, g, i, c],
            device_id={"seq": partner},
            device_id_type=MESH,
        )

    def forward(s, g, finish=False, only=tuple((i, c) for c in range(CUTS) for i in range(2))):
        act = (lambda c: c.wait_send()) if finish else (lambda c: c.start())
        if s + 2 <= back:
            @pl.when((me >= s) & (me + 2 < n))
            def _():
                for i, c in only:
                    act(along(s, g, i, c))

            @pl.when((me >= s) & (odd == 0))
            def _():
                for i, c in only:
                    act(across(s, s // 2 + 1, g, i, c))
        if s >= 2:
            @pl.when((me >= s) & (odd == 1))
            def _():
                for i, c in only:
                    act(across(s, s // 2, g, i, c))

    order_of = tuple((i, c) for c in range(CUTS) for i in range(2))

    def arrive(s, g, only=order_of):
        for i, c in only:
            @pl.when(me >= s)
            def _():
                if s % 2 == 0:
                    along(s - 2, g, i, c).wait_recv()
                else:
                    across(s + 1, (s + 1) // 2, g, i, c).wait_recv()

            if s % 2 == 0:
                forward(s, g, only=((i, c),))

    def attend(s, g, low=0, top_key=None):
        def one_head(head):
            lanes = slice(g * HD, (g + 1) * HD)
            size = math.gcd(tokens, SUB)
            for r in range(0, tokens, size):
                cut = slice(r, r + size)
                first = max(low, (s * tokens + r - reach + 1) // HD * HD)
                last = min(r + size if s == 0 else tokens, top_key or tokens)
                if first >= last:
                    continue
                span = last - first
                queries = q[cut, head * HD:(head + 1) * HD]
                part_of = slice(first, last)
                keys = k[part_of, lanes] if s == 0 else kv[s - 1, g, 0, part_of]
                values = v[part_of, lanes] if s == 0 else kv[s - 1, g, 1, part_of]
                values = jnp.concatenate([values, jnp.ones_like(values)], axis=1)
                scores = dot_t(queries, keys)
                limit = lo[cut]
                if (s + 1) * tokens > NEAR:
                    place = me * tokens + r + lax.broadcasted_iota(jnp.int32, (size, HD), 0)
                    limit = jnp.maximum(limit, place - windows[head] + 1)
                limit = limit - ((me - s) * tokens + first)
                column = lax.broadcasted_iota(jnp.int32, (size, span), 1)
                allowed = column >= wide(limit, span)
                if s == 0:
                    allowed = allowed & (
                        column <= lax.broadcasted_iota(jnp.int32, (size, span), 0) + r
                    )
                scores = jnp.where(allowed, scores, MASKED)
                high = jnp.max(scores, axis=1, keepdims=True) * exp_scale
                high = jnp.broadcast_to(high, (size, HD))
                if s > 0:
                    old = top[head, cut]
                    high = jnp.maximum(high, old)
                weights = jnp.exp2(scores * exp_scale - wide(high, span))
                added = jnp.dot(
                    weights.astype(jnp.bfloat16), values,
                    preferred_element_type=jnp.float32,
                )
                if s > 0:
                    added = added + acc[head, cut] * wide(jnp.exp2(old - high), 2 * HD)
                top[head, cut] = high
                acc[head, cut] = added

        @pl.when(me >= s)
        def _():
            for r in range(per):
                one_head(g * per + r)

    def to_owner(j):
        return [
            pltpu.make_async_remote_copy(
                src_ref=src,
                dst_ref=dst.at[j],
                send_sem=ps.at[i],
                recv_sem=pr.at[j, i],
                device_id={"seq": 0},
                device_id_type=MESH,
            )
            for i, (src, dst) in enumerate(((part, gathered), (stats, gathered_stats)))
        ]

    def decode_partials():
        for i in (2, 3, 4):
            loads[i].wait()
        spread[...] = jnp.zeros_like(spread)
        for head in range(heads):
            g = head // per
            spread[:, head, g * HD:(g + 1) * HD] = (
                dq[:, head * HD:(head + 1) * HD].astype(jnp.float32)
            )
        step = math.gcd(pages, 8)
        lane = lax.broadcasted_iota(jnp.int32, (heads, PAGE), 1)
        group = lax.broadcasted_iota(jnp.int32, (heads, HD), 0) // per

        def block(b, carry):
            levels, owners = carry
            scores, spans, who = [], [], []
            for i in range(step):
                page = order[b * step + i]
                owner = page // pages_request
                left = lengths[owner] - (page - owner * pages_request) * PAGE
                span = pl.ds(pl.multiple_of((b * step + i) * PAGE, PAGE), PAGE)
                score = dot_t(spread[owner].astype(jnp.bfloat16), ckv[span, :])
                scores.append(jnp.where(lane < left, score, MASKED))
                spans.append(span)
                who.append(owner)
            scores = jnp.concatenate(scores, axis=0)
            high = jnp.max(scores, axis=1, keepdims=True)
            high = jnp.broadcast_to(jnp.maximum(high, FLOOR) * exp_scale, scores.shape)
            weights = jnp.exp2(scores * exp_scale - high)
            total = jnp.broadcast_to(jnp.sum(weights, axis=1, keepdims=True), scores.shape)
            some = total > 0.0
            whole = jnp.where(some, total, 1.0)
            level = jnp.where(some, high + jnp.log2(whole), FLOOR)
            weights = (weights / whole).astype(jnp.bfloat16)
            for i in range(step):
                cut = slice(i * heads, (i + 1) * heads)
                both = jnp.dot(
                    weights[cut], cvv[spans[i], :], preferred_element_type=jnp.float32
                )
                mixed = both[:, :HD]
                for g in range(1, groups):
                    mixed = jnp.where(group == g, both[:, g * HD:(g + 1) * HD], mixed)
                pieces[b * step + i] = mixed
                here = lane == b * step + i
                levels = jnp.where(here, level[cut], levels)
                owners = jnp.where(here, who[i].astype(jnp.float32), owners)
            return (levels, owners)

        blank = jnp.zeros((heads, PAGE), jnp.float32)
        levels, owners = lax.fori_loop(
            0, pages // step, block, (blank + FLOOR, blank - 1.0)
        )
        stats[:heads] = levels
        stats[heads:] = owners
        for head in range(heads):
            part[head] = pieces[:, head].astype(jnp.bfloat16)

        @pl.when(me > 0)
        def _():
            for copy in to_owner(me):
                copy.start()

    def decode_merge():
        @pl.when(me == 0)
        def _():
            loads[7].wait()
            loads[8].wait()
            gathered[0] = part[...]
            gathered_stats[0] = stats[...]
            for j in range(1, n):
                for copy in to_owner(j):
                    copy.wait_recv()
            request = lax.broadcasted_iota(jnp.int32, (reqs, PAGE), 0).astype(jnp.float32)

            def one_head(r):
                queries = dq[:, r * HD:(r + 1) * HD].astype(jnp.float32)
                group = slice(r // per * HD, (r // per + 1) * HD)
                own = jnp.sum(queries * dk[:, group].astype(jnp.float32), axis=1, keepdims=True)
                own = jnp.broadcast_to(own * exp_scale, (reqs, HD))
                levels = [
                    jnp.where(
                        gathered_stats[j, heads:heads + 1, :] == request,
                        gathered_stats[j, r:r + 1, :], FLOOR,
                    )
                    for j in range(n)
                ]
                high = functools.reduce(jnp.maximum, levels)
                high = jnp.broadcast_to(jnp.max(high, axis=1, keepdims=True), own.shape)
                high = jnp.maximum(own, high)
                mine = jnp.exp2(own - high)
                weights = [jnp.exp2(level - high) for level in levels]
                count = jnp.sum(sum(weights), axis=1, keepdims=True)
                summed = mine * dv[:, group].astype(jnp.float32)
                for j in range(n):
                    summed = summed + jnp.dot(
                        weights[j][:, :pages].astype(jnp.bfloat16), gathered[j, r],
                        preferred_element_type=jnp.float32,
                    )
                att[r] = (summed / (mine + count)).astype(jnp.bfloat16)

            for r in range(heads):
                one_head(r)

    levels = n // 2
    near = max(levels // 2, 1)

    def finals(level):
        return pltpu.make_async_remote_copy(
            src_ref=att,
            dst_ref=att,
            send_sem=fs.at[level],
            recv_sem=fr.at[0 if level else 1],
            device_id={"seq": 2 * level if level else partner},
            device_id_type=MESH,
        )

    def publish(finish=False):
        act = (lambda c: c.wait_send()) if finish else (lambda c: c.start())

        @pl.when(me == 0)
        def _():
            for level in range(min(near, levels - 1), 0, -1):
                act(finals(level))

    def relay(finish=False):
        act = (lambda c: c.wait_send()) if finish else (lambda c: c.start())
        for level in range(near + 1, levels):
            @pl.when(me == 2 * (level - near + 1))
            def _():
                if not finish:
                    finals(1).wait_recv()
                act(finals(level))

    def share(finish=False):
        relays = range(2, levels - near + 1)

        @pl.when(odd == 0)
        def _():
            if finish:
                finals(0).wait_send()
            else:
                waiting = me >= 2
                for level in relays:
                    waiting = waiting & (me != 2 * level)

                @pl.when(waiting)
                def _():
                    finals(1).wait_recv()

                finals(0).start()

    half = tokens // 2
    half_reqs = reqs // 2
    wide_rows = per * HD
    width = total.shape[2]
    blocks = total.shape[0]

    def borrow(g):
        span = pl.ds(g * wide_rows, wide_rows)
        return pltpu.make_async_remote_copy(
            src_ref=w.at[span],
            dst_ref=wx.at[span],
            send_sem=ws.at[g],
            recv_sem=wr.at[g],
            device_id={"tp": other},
            device_id_type=MESH,
        )

    def exchange(g):
        return pltpu.make_async_remote_copy(
            src_ref=rows.at[g, other],
            dst_ref=incoming.at[g],
            send_sem=ts.at[g],
            recv_sem=tr.at[g],
            device_id={"tp": other},
            device_id_type=MESH,
        )

    def settle(g):
        for r in range(per):
            head = g * per + r
            cut = slice(r * HD, (r + 1) * HD)
            done = (acc[head, :, :HD] / acc[head, :, HD:]).astype(jnp.bfloat16)
            for c in range(2):
                rows[g, c, :half, cut] = done[c * half:(c + 1) * half]
                rows[g, c, half:, cut] = att[head, c * half_reqs:(c + 1) * half_reqs]
        exchange(g).start()

    def project(g, mine):
        weights = wv if mine else wx
        depth = slice(g * wide_rows, (g + 1) * wide_rows)
        first = mine and g == 0
        last = not mine and g == groups - 1

        def block(b, carry):
            span = pl.ds(pl.multiple_of(b * width, width), width)
            left = rows[g, core] if mine else incoming[g]
            added = jnp.dot(left, weights[depth, span], preferred_element_type=jnp.float32)
            if not first:
                added = added + total[b]
            if last:
                out_p[:, span] = added[:half].astype(jnp.bfloat16)
                out_d[:, span] = added[half:].astype(jnp.bfloat16)
            else:
                total[b] = added
            return carry

        lax.fori_loop(0, blocks, block, 0)

    for i in (0, 1):
        loads[i].wait()
    for g in range(groups):
        forward(0, g)
    pass_gate()
    decode_partials()
    for load in loads[7:]:
        load.start()
    for g in range(groups):
        borrow(g).start()
    loads[5].wait()
    position = me * tokens + lax.broadcasted_iota(jnp.int32, (tokens, HD), 0)
    place = position.astype(jnp.float32)
    start = jnp.zeros((tokens, HD), jnp.float32)
    for document in range(1, DOCS):
        before = (docs[...] < document).astype(jnp.float32)
        before = jnp.sum(jnp.sum(before, axis=0, keepdims=True), axis=1, keepdims=True)
        start = jnp.where(before <= place, jnp.maximum(start, before), start)
    lo[...] = start.astype(jnp.int32)
    loads[6].wait()
    steps = [(s, g) for s in range(2, back + 1, 2) for g in range(groups)]
    arrive(*steps[0], order_of[:1])
    for g in range(groups):
        attend(0, g)
        if g == 0:
            arrive(*steps[0], order_of[1:2])
    decode_merge()
    publish()

    def early():
        @pl.when(odd == 1)
        def _():
            finals(0).wait_recv()

        settle(0)
        loads[9].wait()
        project(0, True)
        for i in range(groups):
            borrow(i).wait_recv()
        exchange(0).wait_recv()
        if groups > 1:
            project(0, False)

    for step, (s, g) in enumerate(steps):
        later = steps[step + 1:step + 2]
        arrive(s, g, order_of[2:])
        attend(s, g)
        for following in later:
            arrive(*following, order_of[:1])
        if not later:
            pl.when(odd == 0)(early)
            for c in range(CUTS):
                arrive(s - 1, g, order_of[2 * c:2 * c + 2])
                attend(s - 1, g, c * piece, (c + 1) * piece)
            pl.when(odd == 1)(early)
        else:
            arrive(s - 1, g)
            attend(s - 1, g)
        for following in later:
            arrive(*following, order_of[1:2])
        if s == 2 and g == groups - 1:
            relay()
        if s == back and g == 0:
            share()
    for g in range(1, groups):
        settle(g)
        project(g, True)
        exchange(g).wait_recv()
        if g < groups - 1:
            project(g, False)
    project(groups - 1, False)

    for g in range(groups):
        exchange(g).wait_send()
        borrow(g).wait_send()
    for s in range(0, back + 1, 2):
        for g in range(groups):
            forward(s, g, finish=True)
    @pl.when(me > 0)
    def _():
        for copy in to_owner(me):
            copy.wait_send()
        loads[7].wait()
        loads[8].wait()

    publish(True)
    relay(True)
    share(True)


def on_device(
    n, prefill_query, prefill_key, prefill_value, doc_ids, head_window, dec_query, dec_key,
    dec_value, cache_key, cache_value, page_order, lengths, out_proj,
):
    tokens, width = prefill_query.shape
    heads = width // HD
    groups = prefill_key.shape[1] // HD
    reqs = dec_query.shape[0]
    model = out_proj.shape[1]
    pages = page_order.shape[0]
    reach = min(doc_ids.shape[0] // 2, WINDOW)
    back = -(-reach // tokens)
    back += back % 2

    pages_request = page_order.shape[0] * n // reqs
    docs = doc_ids.reshape(-1, HD)
    vmem = pl.BlockSpec(memory_space=pltpu.VMEM)
    hbm = pl.BlockSpec(memory_space=pltpu.HBM)
    smem = pl.BlockSpec(memory_space=pltpu.SMEM)
    block = 1024
    blocks = model // block
    merged = (tokens + reqs) // 2
    dma = pltpu.SemaphoreType.DMA
    args = (
        prefill_query, prefill_key, prefill_value, docs, head_window, page_order, lengths,
        dec_query, dec_key, dec_value, cache_key, cache_value, out_proj,
    )
    result = pl.pallas_call(
        functools.partial(kernel, n, back, reach, pages_request),
        out_shape=(
            jax.ShapeDtypeStruct((tokens // 2, model), jnp.bfloat16),
            jax.ShapeDtypeStruct((reqs // 2, model), jnp.bfloat16),
        ),
        in_specs=[hbm] * 4 + [smem] * 3 + [hbm] * 6,
        out_specs=(vmem, vmem),
        scratch_shapes=[
            pltpu.VMEM(prefill_query.shape, jnp.bfloat16),
            pltpu.VMEM(prefill_key.shape, jnp.bfloat16),
            pltpu.VMEM(prefill_value.shape, jnp.bfloat16),
            pltpu.VMEM(docs.shape, jnp.int32),
            pltpu.VMEM(dec_query.shape, jnp.bfloat16),
            pltpu.VMEM(dec_key.shape, jnp.bfloat16),
            pltpu.VMEM(dec_value.shape, jnp.bfloat16),
            pltpu.VMEM((back, groups, 2, tokens, HD), jnp.bfloat16),
            pltpu.VMEM((heads, tokens, HD), jnp.float32),
            pltpu.VMEM((heads, tokens, 2 * HD), jnp.float32),
            pltpu.VMEM((tokens, HD), jnp.int32),
            pltpu.VMEM((groups, 2, merged, heads // groups * HD), jnp.bfloat16),
            pltpu.VMEM(cache_key.shape, jnp.bfloat16),
            pltpu.VMEM(cache_value.shape, jnp.bfloat16),
            pltpu.VMEM(out_proj.shape, jnp.bfloat16),
            pltpu.VMEM((reqs, heads, groups * HD), jnp.float32),
            pltpu.VMEM((pages, heads, HD), jnp.float32),
            pltpu.VMEM((heads, pages, HD), jnp.bfloat16),
            pltpu.VMEM((2 * heads, PAGE), jnp.float32),
            pltpu.VMEM((n, heads, pages, HD), jnp.bfloat16),
            pltpu.VMEM((n, 2 * heads, PAGE), jnp.float32),
            pltpu.VMEM((heads, reqs, HD), jnp.bfloat16),
            pltpu.VMEM((blocks, merged, block), jnp.float32),
            pltpu.VMEM(out_proj.shape, jnp.bfloat16),
            pltpu.VMEM((groups, merged, heads // groups * HD), jnp.bfloat16),
            dma((10,)),
            dma((back // 2, groups, 2, CUTS)),
            dma((back // 2, groups, 2, CUTS)),
            dma((back // 2, groups, 2, CUTS)),
            dma((back // 2, groups, 2, CUTS)),
            dma((2,)),
            dma((n, 2)),
            dma((n // 2,)),
            dma((2,)),
            dma((groups,)),
            dma((groups,)),
            dma((groups,)),
            dma((groups,)),
            pltpu.SemaphoreType.REGULAR,
        ],
        compiler_params=pltpu.CompilerParams(
            collective_id=0, has_side_effects=True, vmem_limit_bytes=48 * 1024 * 1024
        ),
    )(*[pltpu.with_memory_space_constraint(x, pltpu.HBM) for x in args])
    return pl.pallas_call(
        put,
        out_shape=tuple(jax.ShapeDtypeStruct(x.shape, x.dtype) for x in result),
        in_specs=[vmem, vmem],
        out_specs=(hbm, hbm),
        scratch_shapes=[dma((2,))],
        compiler_params=pltpu.CompilerParams(vmem_limit_bytes=4 * 1024 * 1024),
    )(*result)


def solution(mesh):
    placed = (
        P(("rep", "seq"), "tp"),
        P(("rep", "seq"), "tp"),
        P(("rep", "seq"), "tp"),
        P("rep"),
        P("tp"),
        P("rep", "tp"),
        P("rep", "tp"),
        P("rep", "tp"),
        P(("rep", "seq"), "tp"),
        P(("rep", "seq"), "tp"),
        P(("rep", "seq")),
        P("rep"),
        P("tp", None),
    )
    return jax.shard_map(
        functools.partial(on_device, mesh.shape["seq"]),
        mesh=mesh,
        in_specs=placed,
        out_specs=(P(("rep", "seq", "tp"), None), P(("rep", "tp"), None)),
        check_vma=False,
    )
```

time: 50.6 us -> 44.3 us (0.88)
  Pallas kernels: 49.1 us -> 43.3 us
    pallas_call x1, Pallas kernels: 47.7 us -> 41.9 us  [on_device(): pl.pallas_call(functools.partial(kernel, n, back, reach, pages_request),...]
where the time goes in v1:
time: 44.3 us; the launch traced here: 44.1 us
  Pallas kernels  43.3 us (98%)
  between operations  0.8 us (2%)
    pallas_call x1, Pallas kernels, on_device(): pl.pallas_call(functools.partial(kernel, n, back, reach, pages_request),...  41.9 us
    pallas_call x1, Pallas kernels, on_device(): pl.pallas_call(put, out_shape=tuple((jax.ShapeDtypeStruct(x.shape, x.dtyp...  1.41 us

profile of v1, /device:TPU:16, one launch (start us, length us, event | category | flops | bytes accessed | tf_op | source)
XLA Modules:
  0.0 44.1 jit_solution(10935681602867622996)
XLA Ops:
  0.6 41.9 %shard_map.140 = (bf16[256,4096]{1,0:T(8,128)(2,1)S(1)}, bf16[32,4096]{1,0:T(8,128)(2,1)S(1)}) custom-call(bf16[512,1024]{1,0:T(8,128)(2,1)} %q_hbm.1, bf16[512,256]{1,0:T(8,128)(2,1)} %k_hbm.1, bf16[512,256]{1,0:T(8,128)(2,1)} %v_hbm.1, s32[32,128]{1,0:T(8,128)} %bitcast.1, s32[8]{0:T(128)} %windows.1, s32[32]{0:T(128)} %order.1, s32[64]{0:T(128)} %lengths.1, ...), custom_call_target="tpu_custom_call" | custom-call | tf_op jit(solution)/shard_map/pallas_call | solution.py:540
  42.5 1.4 %shard_map.141 = (bf16[256,4096]{1,0:T(8,128)(2,1)}, bf16[32,4096]{1,0:T(8,128)(2,1)}) custom-call(bf16[256,4096]{1,0:T(8,128)(2,1)S(1)} %get-tuple-element.4.block_p, bf16[32,4096]{1,0:T(8,128)(2,1)S(1)} %get-tuple-element.5.block_d), custom_call_target="tpu_custom_call" | custom-call | tf_op jit(solution)/shard_map/pallas_call | solution.py:593

commit v2 on v1

--- a/solution.py
+++ b/solution.py
@@ -198,17 +198,21 @@
             for r in range(per):
                 one_head(g * per + r)
 
-    def to_owner(j):
+    def to_owner(j, g):
+        span = pl.ds(g * per, per)
+        sends = [(part.at[span], gathered.at[j, span])]
+        if g == 0:
+            sends.insert(0, (stats, gathered_stats.at[j]))
         return [
             pltpu.make_async_remote_copy(
                 src_ref=src,
-                dst_ref=dst.at[j],
-                send_sem=ps.at[i],
-                recv_sem=pr.at[j, i],
+                dst_ref=dst,
+                send_sem=ps.at[g + i * groups],
+                recv_sem=pr.at[j, g + i * groups],
                 device_id={"seq": 0},
                 device_id_type=MESH,
             )
-            for i, (src, dst) in enumerate(((part, gathered), (stats, gathered_stats)))
+            for i, (src, dst) in enumerate(reversed(sends))
         ]
 
     def decode_partials():
@@ -270,8 +274,52 @@
 
         @pl.when(me > 0)
         def _():
-            for copy in to_owner(me):
-                copy.start()
+            for g in range(groups):
+                for copy in to_owner(me, g):
+                    copy.start()
+
+    levels = n // 2
+    near = max(levels // 2, 1)
+
+    def finals(level, g):
+        span = pl.ds(g * per, per)
+        return pltpu.make_async_remote_copy(
+            src_ref=att.at[span],
+            dst_ref=att.at[span],
+            send_sem=fs.at[level, g],
+            recv_sem=fr.at[0 if level else 1, g],
+            device_id={"seq": 2 * level if level else partner},
+            device_id_type=MESH,
+        )
+
+    def publish(g, finish=False):
+        for level in range(min(near, levels - 1), -1, -1):
+            if finish:
+                finals(level, g).wait_send()
+            else:
+                finals(level, g).start()
+
+    relays = range(2, levels - near + 1)
+
+    def relay(g):
+        for level in range(near + 1, levels):
+            @pl.when(me == 2 * (level - near + 1))
+            def _():
+                finals(1, g).wait_recv()
+                finals(level, g).start()
+
+    def share(g):
+        waiting = (odd == 0) & (me >= 2)
+        for level in relays:
+            waiting = waiting & (me != 2 * level)
+
+        @pl.when(waiting)
+        def _():
+            finals(1, g).wait_recv()
+
+        @pl.when((odd == 0) & (me >= 2))
+        def _():
+            finals(0, g).start()
 
     def decode_merge():
         @pl.when(me == 0)
@@ -280,9 +328,6 @@
             loads[8].wait()
             gathered[0] = part[...]
             gathered_stats[0] = stats[...]
-            for j in range(1, n):
-                for copy in to_owner(j):
-                    copy.wait_recv()
             request = lax.broadcasted_iota(jnp.int32, (reqs, PAGE), 0).astype(jnp.float32)
 
             def one_head(r):
@@ -311,56 +356,13 @@
                     )
                 att[r] = (summed / (mine + count)).astype(jnp.bfloat16)
 
-            for r in range(heads):
-                one_head(r)
-
-    levels = n // 2
-    near = max(levels // 2, 1)
-
-    def finals(level):
-        return pltpu.make_async_remote_copy(
-            src_ref=att,
-            dst_ref=att,
-            send_sem=fs.at[level],
-            recv_sem=fr.at[0 if level else 1],
-            device_id={"seq": 2 * level if level else partner},
-            device_id_type=MESH,
-        )
-
-    def publish(finish=False):
-        act = (lambda c: c.wait_send()) if finish else (lambda c: c.start())
-
-        @pl.when(me == 0)
-        def _():
-            for level in range(min(near, levels - 1), 0, -1):
-                act(finals(level))
-
-    def relay(finish=False):
-        act = (lambda c: c.wait_send()) if finish else (lambda c: c.start())
-        for level in range(near + 1, levels):
-            @pl.when(me == 2 * (level - near + 1))
-            def _():
-                if not finish:
-                    finals(1).wait_recv()
-                act(finals(level))
-
-    def share(finish=False):
-        relays = range(2, levels - near + 1)
-
-        @pl.when(odd == 0)
-        def _():
-            if finish:
-                finals(0).wait_send()
-            else:
-                waiting = me >= 2
-                for level in relays:
-                    waiting = waiting & (me != 2 * level)
-
-                @pl.when(waiting)
-                def _():
-                    finals(1).wait_recv()
-
-                finals(0).start()
+            for g in range(groups):
+                for j in range(1, n):
+                    for copy in to_owner(j, g):
+                        copy.wait_recv()
+                for r in range(g * per, (g + 1) * per):
+                    one_head(r)
+                publish(g)
 
     half = tokens // 2
     half_reqs = reqs // 2
@@ -447,16 +449,19 @@
         if g == 0:
             arrive(*steps[0], order_of[1:2])
     decode_merge()
-    publish()
+
+    def obtain(g):
+        @pl.when(odd == 1)
+        def _():
+            finals(0, g).wait_recv()
 
     def early():
-        @pl.when(odd == 1)
-        def _():
-            finals(0).wait_recv()
-
+        obtain(0)
         settle(0)
         loads[9].wait()
         project(0, True)
+
+    def middle():
         for i in range(groups):
             borrow(i).wait_recv()
         exchange(0).wait_recv()
@@ -470,21 +475,39 @@
         for following in later:
             arrive(*following, order_of[:1])
         if not later:
-            pl.when(odd == 0)(early)
-            for c in range(CUTS):
-                arrive(s - 1, g, order_of[2 * c:2 * c + 2])
-                attend(s - 1, g, c * piece, (c + 1) * piece)
-            pl.when(odd == 1)(early)
+            for i in range(1, groups):
+                share(i)
+
+            @pl.when(odd == 0)
+            def _():
+                if step == 0 or groups == 1:
+                    early()
+                middle()
+
+            arrive(s - 1, g)
+            attend(s - 1, g)
+
+            @pl.when(odd == 1)
+            def _():
+                early()
+                middle()
+
         else:
+            if s == back and g == 0:
+                for i in range(1, groups):
+                    relay(i)
             arrive(s - 1, g)
             attend(s - 1, g)
         for following in later:
             arrive(*following, order_of[1:2])
         if s == 2 and g == groups - 1:
-            relay()
+            relay(0)
         if s == back and g == 0:
-            share()
+            share(0)
+            if groups > 1:
+                pl.when(odd == 0)(early)
     for g in range(1, groups):
+        obtain(g)
         settle(g)
         project(g, True)
         exchange(g).wait_recv()
@@ -500,14 +523,25 @@
             forward(s, g, finish=True)
     @pl.when(me > 0)
     def _():
-        for copy in to_owner(me):
-            copy.wait_send()
+        for g in range(groups):
+            for copy in to_owner(me, g):
+                copy.wait_send()
         loads[7].wait()
         loads[8].wait()
 
-    publish(True)
-    relay(True)
-    share(True)
+    for g in range(groups):
+        @pl.when(me == 0)
+        def _():
+            publish(g, True)
+
+        for level in range(near + 1, levels):
+            @pl.when(me == 2 * (level - near + 1))
+            def _():
+                finals(level, g).wait_send()
+
+        @pl.when((odd == 0) & (me >= 2))
+        def _():
+            finals(0, g).wait_send()
 
 
 def on_device(
@@ -529,7 +563,7 @@
     vmem = pl.BlockSpec(memory_space=pltpu.VMEM)
     hbm = pl.BlockSpec(memory_space=pltpu.HBM)
     smem = pl.BlockSpec(memory_space=pltpu.SMEM)
-    block = 1024
+    block = 4096
     blocks = model // block
     merged = (tokens + reqs) // 2
     dma = pltpu.SemaphoreType.DMA
@@ -576,10 +610,10 @@
             dma((back // 2, groups, 2, CUTS)),
             dma((back // 2, groups, 2, CUTS)),
             dma((back // 2, groups, 2, CUTS)),
-            dma((2,)),
-            dma((n, 2)),
-            dma((n // 2,)),
-            dma((2,)),
+            dma((groups + 1,)),
+            dma((n, groups + 1)),
+            dma((n // 2, groups)),
+            dma((2, groups)),
             dma((groups,)),
             dma((groups,)),
             dma((groups,)),

time: 44.3 us -> 42.5 us (0.959)
  Pallas kernels: 43.3 us -> 41.1 us
    pallas_call x1, Pallas kernels: 41.9 us -> 39.7 us  [on_device(): pl.pallas_call(functools.partial(kernel, n, back, reach, pages_request),...]
where the time goes in v2:
time: 42.5 us; the launch traced here: 41.9 us
  Pallas kernels  41.1 us (97%)
  between operations  0.82 us (2%)
    pallas_call x1, Pallas kernels, on_device(): pl.pallas_call(functools.partial(kernel, n, back, reach, pages_request),...  39.7 us
    pallas_call x1, Pallas kernels, on_device(): pl.pallas_call(put, out_shape=tuple((jax.ShapeDtypeStruct(x.shape, x.dtyp...  1.41 us

profile of v2, /device:TPU:16, one launch (start us, length us, event | category | flops | bytes accessed | tf_op | source)
XLA Modules:
  0.0 41.9 jit_solution(4998811669944816085)
XLA Ops:
  0.6 39.7 %shard_map.140 = (bf16[256,4096]{1,0:T(8,128)(2,1)S(1)}, bf16[32,4096]{1,0:T(8,128)(2,1)S(1)}) custom-call(bf16[512,1024]{1,0:T(8,128)(2,1)} %q_hbm.1, bf16[512,256]{1,0:T(8,128)(2,1)} %k_hbm.1, bf16[512,256]{1,0:T(8,128)(2,1)} %v_hbm.1, s32[32,128]{1,0:T(8,128)} %bitcast.1, s32[8]{0:T(128)} %windows.1, s32[32]{0:T(128)} %order.1, s32[64]{0:T(128)} %lengths.1, ...), custom_call_target="tpu_custom_call" | custom-call | tf_op jit(solution)/shard_map/pallas_call | solution.py:574
  40.3 1.4 %shard_map.141 = (bf16[256,4096]{1,0:T(8,128)(2,1)}, bf16[32,4096]{1,0:T(8,128)(2,1)}) custom-call(bf16[256,4096]{1,0:T(8,128)(2,1)S(1)} %get-tuple-element.4.block_p, bf16[32,4096]{1,0:T(8,128)(2,1)S(1)} %get-tuple-element.5.block_d), custom_call_target="tpu_custom_call" | custom-call | tf_op jit(solution)/shard_map/pallas_call | solution.py:627

commit v3 on v2

--- a/solution.py
+++ b/solution.py
@@ -67,8 +67,8 @@
         (dk_hbm, dk), (dv_hbm, dv), (w, wv),
     )
     loads = [pltpu.make_async_copy(a, b, local_sem.at[i]) for i, (a, b) in enumerate(pairs)]
-    for load in loads[:7]:
-        load.start()
+    for i in (0, 1, 2, 5, 6):
+        loads[i].start()
 
     barrier = pltpu.get_barrier_semaphore()
 
@@ -426,12 +426,8 @@
         loads[i].wait()
     for g in range(groups):
         forward(0, g)
-    pass_gate()
-    decode_partials()
-    for load in loads[7:]:
-        load.start()
-    for g in range(groups):
-        borrow(g).start()
+    for i in (3, 4):
+        loads[i].start()
     loads[5].wait()
     position = me * tokens + lax.broadcasted_iota(jnp.int32, (tokens, HD), 0)
     place = position.astype(jnp.float32)
@@ -443,11 +439,16 @@
     lo[...] = start.astype(jnp.int32)
     loads[6].wait()
     steps = [(s, g) for s in range(2, back + 1, 2) for g in range(groups)]
-    arrive(*steps[0], order_of[:1])
     for g in range(groups):
         attend(0, g)
         if g == 0:
-            arrive(*steps[0], order_of[1:2])
+            pass_gate()
+            decode_partials()
+            for load in loads[7:]:
+                load.start()
+            for g in range(groups):
+                borrow(g).start()
+            arrive(*steps[0], order_of[:2])
     decode_merge()
 
     def obtain(g):

time: 42.5 us -> 43.8 us (1.031)
  the two profiles are of different devices: /device:TPU:16 before, /device:TPU:27 now
where the time goes in v3:
time: 43.8 us; the launch traced here: 43.6 us
  Pallas kernels  42.8 us (98%)
  between operations  0.82 us (2%)
    pallas_call x1, Pallas kernels, on_device(): pl.pallas_call(functools.partial(kernel, n, back, reach, pages_request),...  41.4 us
    pallas_call x1, Pallas kernels, on_device(): pl.pallas_call(put, out_shape=tuple((jax.ShapeDtypeStruct(x.shape, x.dtyp...  1.41 us

profile of v3, /device:TPU:27, one launch (start us, length us, event | category | flops | bytes accessed | tf_op | source)
XLA Modules:
  0.0 43.6 jit_solution(17219641144040748525)
XLA Ops:
  0.6 41.4 %shard_map.140 = (bf16[256,4096]{1,0:T(8,128)(2,1)S(1)}, bf16[32,4096]{1,0:T(8,128)(2,1)S(1)}) custom-call(bf16[512,1024]{1,0:T(8,128)(2,1)} %q_hbm.1, bf16[512,256]{1,0:T(8,128)(2,1)} %k_hbm.1, bf16[512,256]{1,0:T(8,128)(2,1)} %v_hbm.1, s32[32,128]{1,0:T(8,128)} %bitcast.1, s32[8]{0:T(128)} %windows.1, s32[32]{0:T(128)} %order.1, s32[64]{0:T(128)} %lengths.1, ...), custom_call_target="tpu_custom_call" | custom-call | tf_op jit(solution)/shard_map/pallas_call | solution.py:575
  42.0 1.4 %shard_map.141 = (bf16[256,4096]{1,0:T(8,128)(2,1)}, bf16[32,4096]{1,0:T(8,128)(2,1)}) custom-call(bf16[256,4096]{1,0:T(8,128)(2,1)S(1)} %get-tuple-element.4.block_p, bf16[32,4096]{1,0:T(8,128)(2,1)S(1)} %get-tuple-element.5.block_d), custom_call_target="tpu_custom_call" | custom-call | tf_op jit(solution)/shard_map/pallas_call | solution.py:628
